TPU v7x, 256 devices: a whole 4x4x8 slice. The times are simulated.
256 devices in a mesh: docs: 64 (over x, z, core), rep: 4 (over y).
Axes of the slice: x: 4, y: 4, z: 8, core: 2. Of those that a mesh axis runs over, the one named last changes fastest.
Arguments:
- embeddings: bfloat16 [262144, 4096], P(('docs', 'rep')), may hold values from -6 to 6
- pca_basis: bfloat16 [4096, 256], replicated, may hold values from -0.09375 to 0.09375
- cluster: int32 [262144, 1], P(('docs', 'rep')), may hold values from 0 to 255; in each aligned block of 1024 rows (0 to 1023, 1024 to 2047, ...) at most 8 rows name the same one
- doc_index: int32 [262144], P(('docs', 'rep')), may hold values from 0 to 262143, each once
Outputs:
- nearest_sim: float32 [262144], P(('docs', 'rep'))
Inputs may be any that keep to these rules, and one draw needn't show every extreme that they name: In each device's block of 1024 rows no cluster is named by more than 8 rows, a bound that some block reaches. `doc_index`: each document number appears once.
All inputs are finite; a program needn't handle non-finite values.
Results may differ from a plain program's by a relative error of at most 0.0014.
Values may be sent and summed in bfloat16 or wider, within the bound.
A program may use at most 64 MiB of HBM per device.

v0:
```python
import jax
import jax.numpy as jnp
from jax import lax
from jax.sharding import PartitionSpec as P

CL_DEV = 4


sentinel_index = 2**30


def in_blocks(x, dim, size):
    dims = x.shape
    pieces = x.reshape(*dims[:dim], size, dims[dim] // size, *dims[dim + 1 :])
    return jnp.moveaxis(pieces, dim, 0)


def joined_along(pieces, dim):
    pieces = jnp.moveaxis(pieces, 0, dim)
    dims = pieces.shape
    return pieces.reshape(*dims[:dim], dims[dim] * dims[dim + 1], *dims[dim + 2 :])


def exchange_both(x, axis, axes, splits, concats):
    sizes = [lax.axis_size(a) for a in axes]
    pieces = in_blocks(x, splits[0], sizes[0])
    pieces = jnp.moveaxis(in_blocks(pieces, splits[1] + 1, sizes[1]), 0, 1)
    inside = pieces.shape[2:]
    pieces = pieces.reshape(-1, *inside)
    pieces = lax.all_to_all(pieces, axis, split_axis=0, concat_axis=0, tiled=True)
    pieces = joined_along(pieces.reshape(*sizes, *inside), concats[0] + 1)
    return joined_along(pieces, concats[1])


def on_device(embeddings, pca_basis, cluster, doc_index):
    n_docs = lax.axis_size("docs")
    n_rep = lax.axis_size("rep")
    doc_rows = embeddings.shape[0]
    features = pca_basis.shape[1]
    slot_depth = max(2, 2 * doc_rows // (CL_DEV * n_docs))
    clusters = CL_DEV * n_docs
    projected = jnp.dot(embeddings, pca_basis, preferred_element_type=jnp.float32)
    unit_rows = (
        projected * lax.rsqrt(jnp.sum(projected * projected, axis=1, keepdims=True) + 1e-06)
    ).astype(jnp.bfloat16)
    cluster_id = cluster[:, 0]
    one_hot = (cluster_id[:, None] == jnp.arange(clusters, dtype=jnp.int32)[None, :]).astype(
        jnp.bfloat16
    )
    positions = jnp.arange(doc_rows, dtype=jnp.int32)
    before = (positions[None, :] < positions[:, None]).astype(jnp.bfloat16)
    earlier = jnp.dot(before, one_hot, preferred_element_type=jnp.float32)
    member_rank = jnp.sum(earlier * one_hot.astype(jnp.float32), axis=1).astype(jnp.int32)
    slot_of = cluster_id * slot_depth + member_rank
    send_rows = (
        jnp.zeros((clusters * slot_depth, features), jnp.bfloat16).at[slot_of].set(unit_rows)
    )
    send_index = (
        jnp.full((clusters * slot_depth,), sentinel_index, jnp.int32).at[slot_of].set(doc_index)
    )
    per_rep = CL_DEV // n_rep
    recv_rows, recv_index = (
        exchange_both(
            send_rows.reshape(n_docs, n_rep, per_rep * slot_depth, features),
            ("docs", "rep"),
            ("docs", "rep"),
            (0, 1),
            (0, 1),
        ),
        exchange_both(
            send_index.reshape(n_docs, n_rep, per_rep * slot_depth),
            ("docs", "rep"),
            ("docs", "rep"),
            (0, 1),
            (0, 1),
        ),
    )
    member_rows = jnp.moveaxis(
        recv_rows.reshape(n_docs, n_rep, per_rep, slot_depth, features), 2, 0
    ).reshape(per_rep, -1, features)
    member_index = jnp.moveaxis(
        recv_index.reshape(n_docs, n_rep, per_rep, slot_depth), 2, 0
    ).reshape(per_rep, -1)

    def within(inputs):
        rows_here, index_here = inputs
        scores = jnp.einsum("ip,jp->ij", rows_here, rows_here, preferred_element_type=jnp.float32)
        allowed = index_here[None, :] < index_here[:, None]
        return jnp.max(jnp.where(allowed, scores, -1.0), axis=1)

    found = lax.map(within, (member_rows, member_index))
    found = jnp.moveaxis(found.reshape(per_rep, n_docs, n_rep, slot_depth), 0, 2).reshape(
        n_docs, n_rep, per_rep * slot_depth
    )
    returned = exchange_both(found, ("docs", "rep"), ("docs", "rep"), (0, 1), (0, 1))
    nearest = returned.reshape(-1)[slot_of]
    return nearest


def solution(mesh):
    return jax.shard_map(
        on_device,
        mesh=mesh,
        in_specs=(P(("docs", "rep"), None), P(), P(("docs", "rep"), None), P(("docs", "rep"))),
        out_specs=P(("docs", "rep")),
        check_vma=False,
    )
```

profile of v0, /device:TPU:1, one launch (start us, length us, event | category | flops | bytes accessed | tf_op | source)
XLA Modules:
  0.0 114.4 jit_solution(14217634011258486768)
XLA Ops:
  0.0 0.0 copy-start
  0.0 1.6 %fusion.2 = f32[1024]{0:T(1024)S(1)} fusion(s32[1024]{0:T(1024)} %bitcast.45), kind=kOutput, calls=%fused_computation.7 | convolution fusion | flops 539491328 | bytes 8192 | tf_op jit(solution)/shard_map/dot_general | solution.py:52
  1.7 0.7 compare_select_fusion
  2.4 4.5 %scatter_custom_fusion = s32[2048]{0:T(1024)S(1)} fusion(s32[1024]{0:T(1024)S(1)} %bitcast.41, s32[1024]{0:T(1024)} %param.7, s32[]{:T(128)} %constant.9.clone.1), kind=kCustom, calls=%fused_computation.18 | custom fusion | bytes 8704 | tf_op jit(solution)/shard_map/scatter | solution.py:59
  6.8 0.7 reshape_transpose_transpose_reshape_reshape_reshape.6
  7.6 15.6 %all-to-all-start = ((s32[256,1,1,8]{3,2,1,0:T(1,128)}), s32[256,1,1,8]{3,2,1,0:T(1,128)S(1)}, u32[]{:S(2)}, u32[]{:S(2)}) async-start(s32[256,1,1,8]{3,2,1,0:T(1,128)} %bitcast.3), calls=%async_computation | async-start | bytes 262144 | tf_op jit(solution)/shard_map/all_to_all | solution.py:30
  23.2 0.0 copy-done
  23.2 5.8 %multiply_reduce_fusion = (f32[1024]{0:T(1024)S(1)}, f32[1024,256]{0,1:T(8,128)S(1)}) fusion(bf16[1024,4096]{1,0:T(8,128)(2,1)} %param.4, bf16[4096,256]{1,0:T(8,128)(2,1)S(1)} %copy-done), kind=kOutput, calls=%fused_computation.10 | convolution fusion | flops 2148006912 | bytes 11538432 | tf_op jit(solution)/shard_map/dot_general | solution.py:42
  29.0 0.1 multiply_convert_fusion
  29.1 0.2 copy.7
  29.3 6.0 %scatter_custom_fusion.1 = bf16[2048,256]{1,0:T(8,128)(2,1)} fusion(s32[1024]{0:T(1024)S(1)} %bitcast.42, bf16[1024,256]{1,0:T(8,128)(2,1)S(1)} %copy.7, bf16[]{:T(256)} %constant.14.clone.1), kind=kCustom, calls=%fused_computation.13 | custom fusion | bytes 1048578 | tf_op jit(solution)/shard_map/scatter | solution.py:56
  35.4 0.7 all-to-all-done
  36.0 13.1 %all-to-all-start.1 = ((bf16[256,1,1,8,256]{4,3,2,1,0:T(8,128)(2,1)}), bf16[256,1,1,8,256]{4,3,2,1,0:T(8,128)(2,1)S(1)}, u32[]{:S(2)}, u32[]{:S(2)}) async-start(bf16[256,1,1,8,256]{4,3,2,1,0:T(8,128)(2,1)} %bitcast.9), calls=%async_computation.1 | async-start | bytes 2097152 | tf_op jit(solution)/shard_map/all_to_all | solution.py:30
  49.1 0.2 lt.46
  49.3 32.3 %all-to-all-done.1 = bf16[256,1,1,8,256]{4,3,2,1,0:T(8,128)(2,1)S(1)} async-done(((bf16[256,1,1,8,256]{4,3,2,1,0:T(8,128)(2,1)}), bf16[256,1,1,8,256]{4,3,2,1,0:T(8,128)(2,1)S(1)}, u32[]{:S(2)}, u32[]{:S(2)}) %all-to-all-start.1) | async-done | bytes 1048608 | tf_op jit(solution)/shard_map/all_to_all | solution.py:30
  81.5 2.7 %select_reduce_fusion = f32[2048]{0:T(1024)S(1)} fusion(s32[2048]{0:T(1024)S(1)} %lt.46, bf16[256,1,1,8,256]{4,3,2,1,0:T(8,128)(2,1)S(1)} %all-to-all-done.1), kind=kOutput, calls=%fused_computation.3 | convolution fusion | flops 2160064512 | bytes 1064960 | tf_op jit(solution)/shard_map/while/body/eval_jaxpr/ip,jp->ij/dot_general | solution.py:87
  84.2 0.7 reshape_transpose_transpose_reshape_reshape_reshape_transpose_reshape.3
  84.9 5.8 %all-to-all-start.2 = ((f32[256,1,1,8]{3,2,1,0:T(1,128)}), f32[256,1,1,8]{3,2,1,0:T(1,128)S(1)}, u32[]{:S(2)}, u32[]{:S(2)}) async-start(f32[256,1,1,8]{3,2,1,0:T(1,128)} %bitcast.15), calls=%async_computation.2 | async-start | bytes 262144 | tf_op jit(solution)/shard_map/all_to_all | solution.py:30
  90.8 12.9 %all-to-all-done.2 = f32[256,1,1,8]{3,2,1,0:T(1,128)S(1)} async-done(((f32[256,1,1,8]{3,2,1,0:T(1,128)}), f32[256,1,1,8]{3,2,1,0:T(1,128)S(1)}, u32[]{:S(2)}, u32[]{:S(2)}) %all-to-all-start.2) | async-done | bytes 8224 | tf_op jit(solution)/shard_map/all_to_all | solution.py:30
  103.7 0.2 reshape_reshape.3
  103.9 10.5 %gather_fusion = f32[1024]{0:T(1024)} fusion(f32[2048]{0:T(1024)S(1)} %reshape_reshape.3, s32[1024]{0:T(1024)S(1)} %broadcast_clamp_fusion), kind=kCustom, calls=%fused_computation | custom fusion | bytes 12288 | tf_op jit(solution)/shard_map/gather | solution.py:96
  (3 shorter events, 0.0 us)
Async XLA Ops:
  0.0 23.2 %copy-start = (bf16[4096,256]{1,0:T(8,128)(2,1)S(1)}, bf16[4096,256]{1,0:T(8,128)(2,1)}, u32[]{:S(2)}) copy-start(bf16[4096,256]{1,0:T(8,128)(2,1)} %param.5) | copy-start | bytes 6291460
  7.6 28.4 %all-to-all-start = ((s32[256,1,1,8]{3,2,1,0:T(1,128)}), s32[256,1,1,8]{3,2,1,0:T(1,128)S(1)}, u32[]{:S(2)}, u32[]{:S(2)}) async-start(s32[256,1,1,8]{3,2,1,0:T(1,128)} %bitcast.3), calls=%async_computation | async-start | bytes 262144 | tf_op jit(solution)/shard_map/all_to_all | solution.py:30
  36.0 45.5 %all-to-all-start.1 = ((bf16[256,1,1,8,256]{4,3,2,1,0:T(8,128)(2,1)}), bf16[256,1,1,8,256]{4,3,2,1,0:T(8,128)(2,1)S(1)}, u32[]{:S(2)}, u32[]{:S(2)}) async-start(bf16[256,1,1,8,256]{4,3,2,1,0:T(8,128)(2,1)} %bitcast.9), calls=%async_computation.1 | async-start | bytes 2097152 | tf_op jit(solution)/shard_map/all_to_all | solution.py:30
  84.9 18.8 %all-to-all-start.2 = ((f32[256,1,1,8]{3,2,1,0:T(1,128)}), f32[256,1,1,8]{3,2,1,0:T(1,128)S(1)}, u32[]{:S(2)}, u32[]{:S(2)}) async-start(f32[256,1,1,8]{3,2,1,0:T(1,128)} %bitcast.15), calls=%async_computation.2 | async-start | bytes 262144 | tf_op jit(solution)/shard_map/all_to_all | solution.py:30
where the time goes:
time: 115 us; the launch traced here: 114 us
  waiting for transfers between devices  45.8 us (40%)
  starting transfers between devices  34.5 us (30%)
  local copies, waits for them, and re-layouts  23.1 us (20%)
  matrix products  10.1 us (9%)
    all_to_all x3, waiting for transfers between devices, exchange_both(): lax.all_to_all(pieces, axis, split_axis=0, concat_axis=0, tiled=True)  45.8 us
    all_to_all x3, starting transfers between devices, exchange_both(): lax.all_to_all(pieces, axis, split_axis=0, concat_axis=0, tiled=True)  34.5 us
    gather x1, local copies, waits for them, and re-layouts, on_device(): nearest = returned.reshape(-1)[slot_of]  10.5 us
    scatter x1, local copies, waits for them, and re-layouts, on_device(): jnp.zeros((clusters * slot_depth, features), jnp.bfloat16).at[slot_of]  6.03 us
    dot_general x1, matrix products, on_device(): jnp.dot(embeddings, pca_basis, preferred_element_type=jnp.float32)  5.76 us
    scatter x1, local copies, waits for them, and re-layouts, on_device(): jnp.full((clusters * slot_depth,), sentinel_index, jnp.int32).at[slot_of]  4.48 us
    dot_general x1, matrix products, within(): jnp.einsum('ip,jp->ij', rows_here, rows_here, preferred_element_type=jnp....  2.67 us
  transfers between devices with their start and end apart: 3, of which 3 were waited for; matrix products, arithmetic and copies ran while one was open for 11% of the time, Pallas kernels for 0%

commit v1 on v0

v1 whole, which is shorter than its diff:
```python
import jax
import jax.numpy as jnp
from jax import lax
from jax.experimental import pallas as pl
from jax.experimental.pallas import tpu as pltpu
from jax.sharding import PartitionSpec as P

MESH = pl.DeviceIdType.MESH
NX, NY, NZ, NC = 4, 4, 8, 2
NP = NX * NY * NC
DEPTH = 8
ROWS = 1024
PC = 256
E = 4096
BLK = NP * DEPTH
NEMB = 4
EROWS = ROWS // NEMB
ORDER = (4, 3, 5, 2, 6, 1, 7, 0)
BIG = float(2**30)
f32, bf16, i32 = jnp.float32, jnp.bfloat16, jnp.int32


def dot(a, b, ca, cb):
    return lax.dot_general(a, b, (((ca,), (cb,)), ((), ())), preferred_element_type=f32)


def wait_bytes(ref, sem):
    pltpu.make_async_copy(ref, ref, sem).wait()


def kernel(
    cl_ref, ix_ref, emb_ref, bas_ref, out_ref,
    ebuf, bbuf, unit, place, upper, slot_ref, hplane,
    idx_p, idx_in, idx_z, idx_rec, col,
    send, recv1, recv2, rows, best, bestcol,
    ret_row, ret_z, ret_p, ret_c,
    e_sem, b_sem, ip_s, ip_r, iz_s, iz_r, rp_s, rp_r, rz_s, rz_r, bz_s, bz_r, bp_s, bp_r,
):
    d = lax.axis_index("docs")
    y = lax.axis_index("rep")
    core = lax.rem(d, NC)
    z = lax.rem(d // NC, NZ)
    x = d // (NC * NZ)
    p = (x * NY + y) * NC + core

    def at_z(z2):
        return ((x * NZ + z2) * NC + core, y)

    def at_p(p2):
        return (((p2 // (NY * NC)) * NZ + z) * NC + lax.rem(p2, NC), lax.rem(p2 // NC, NY))

    def turn_z(step):
        return lax.rem(z + step, NZ)

    def turn_p(step):
        return lax.rem(p + step, NP)

    barrier = pltpu.get_barrier_semaphore()
    for step in range(1, NZ):
        pl.semaphore_signal(barrier, inc=1, device_id=at_z(turn_z(step)), device_id_type=MESH)

    @pl.loop(1, NP)
    def _(step):
        pl.semaphore_signal(barrier, inc=1, device_id=at_p(turn_p(step)), device_id_type=MESH)

    basis_copy = pltpu.make_async_copy(bas_ref, bbuf, b_sem)
    basis_copy.start()
    emb_copies = [
        pltpu.make_async_copy(emb_ref.at[pl.ds(n * EROWS, EROWS)], ebuf.at[n], e_sem.at[n])
        for n in range(NEMB)
    ]
    for copy in emb_copies:
        copy.start()

    cl = cl_ref[...]
    one_hot = (lax.broadcasted_iota(i32, (NZ * NP, ROWS), 0) == cl).astype(f32)
    upper[...] = (
        lax.broadcasted_iota(i32, (ROWS, ROWS), 0) < lax.broadcasted_iota(i32, (ROWS, ROWS), 1)
    ).astype(f32).astype(bf16)
    earlier = dot(one_hot.astype(bf16), upper[...], 1, 0)
    rank = jnp.sum(earlier * one_hot, axis=0, keepdims=True).astype(i32)
    slot = cl * DEPTH + rank
    slot_ref[...] = slot
    plane = slot // BLK
    inside = lax.rem(slot, BLK)
    place[...] = (lax.broadcasted_iota(i32, (BLK, ROWS), 0) == inside).astype(f32).astype(bf16)
    number = ix_ref[...] + 1
    mine = lax.broadcasted_iota(i32, (128, ROWS), 0) == plane
    total = jnp.zeros((BLK, 128), f32)
    for part, weight in ((number // 4096, 4096.0), (lax.rem(number // 64, 64), 64.0), (lax.rem(number, 64), 1.0)):
        held = jnp.where(mine, part.astype(f32), 0.0).astype(bf16)
        total = total + weight * dot(place[...], held, 1, 1)
    idx_p[...] = total.reshape(NP, DEPTH, 128)

    pl.semaphore_wait(barrier, NZ - 1 + NP - 1)

    @pl.loop(1, NP)
    def _(step):
        p2 = turn_p(step)
        pltpu.make_async_remote_copy(
            src_ref=idx_p.at[p2], dst_ref=idx_in.at[p], send_sem=ip_s, recv_sem=ip_r,
            device_id=at_p(p2), device_id_type=MESH,
        ).start()

    idx_in[p] = idx_p[p]

    basis_copy.wait()

    @pl.loop(0, NEMB)
    def _(n):
        pltpu.make_async_copy(emb_ref.at[pl.ds(n * EROWS, EROWS)], ebuf.at[n], e_sem.at[n]).wait()
        projected = jnp.dot(ebuf[n], bbuf[...], preferred_element_type=f32)
        scale = lax.rsqrt(jnp.sum(projected * projected, axis=1, keepdims=True) + 1e-06)
        unit[pl.ds(pl.multiple_of(n * EROWS, EROWS), EROWS), :] = (projected * scale).astype(bf16)

    for step in ORDER:
        z2 = turn_z(step)
        picks = (lax.broadcasted_iota(i32, (BLK, ROWS), 0) + z2 * BLK == slot_ref[...]).astype(f32)
        chosen = jnp.dot(picks.astype(bf16), unit[...], preferred_element_type=f32)
        send[z2] = chosen.reshape(NP, DEPTH, PC).astype(bf16)

        @pl.loop(1, NP)
        def _(turn, z2=z2):
            p2 = turn_p(turn)
            pltpu.make_async_remote_copy(
                src_ref=send.at[z2, p2], dst_ref=recv1.at[z2, p], send_sem=rp_s, recv_sem=rp_r.at[z2],
                device_id=at_p(p2), device_id_type=MESH,
            ).start()

        recv1[z2, p] = send[z2, p]
        if step == ORDER[0]:
            wait_bytes(idx_in.at[pl.ds(0, NP - 1)], ip_r)
            turned = idx_in[...].reshape(BLK, 128).T
            for k in range(NZ):
                idx_z[k] = turned[k : k + 1, :]
            for k, far in enumerate(ORDER):
                if far:
                    pltpu.make_async_remote_copy(
                        src_ref=idx_z.at[turn_z(far)], dst_ref=idx_rec.at[k], send_sem=iz_s, recv_sem=iz_r,
                        device_id=at_z(turn_z(far)), device_id_type=MESH,
                    ).start()
                else:
                    idx_rec[k] = idx_z[z]

    for k, step in enumerate(ORDER):
        z2 = turn_z(step)
        wait_bytes(recv1.at[z2, pl.ds(0, NP - 1)], rp_r.at[z2])
        if step:
            pltpu.make_async_remote_copy(
                src_ref=recv1.at[z2], dst_ref=recv2.at[k], send_sem=rz_s.at[k], recv_sem=rz_r.at[k],
                device_id=at_z(z2), device_id_type=MESH,
            ).start()

    wait_bytes(idx_rec.at[pl.ds(0, NZ - 1)], iz_r)

    @pl.loop(0, NZ)
    def _(k):
        row = idx_rec[k]
        row = jnp.where(row == 0.0, BIG, row)
        idx_rec[k] = row
        col[k] = jnp.broadcast_to(row, (128, BLK)).T
        best[k] = jnp.full((8, BLK), -1.0, f32)
        bestcol[k] = jnp.full((BLK, 128), -1.0, f32)

    def pair(b, a, same):
        scores = dot(rows[b], rows[a], 1, 1)
        cb = col[b]
        ra = idx_rec[a]
        over_rows = []
        over_cols = None
        for h in range(BLK // 128):
            lanes = slice(h * 128, (h + 1) * 128)
            s = scores[:, lanes]
            allowed = cb < ra[:, lanes]
            over_rows.append(jnp.max(jnp.where(allowed, s, -1.0).reshape(BLK // 8, 8, 128), axis=0))
            if not same:
                other = jnp.where(allowed, -1.0, s)
                over_cols = other if over_cols is None else jnp.maximum(over_cols, other)
        best[a] = jnp.maximum(best[a], jnp.concatenate(over_rows, axis=1))
        if not same:
            bestcol[b] = jnp.maximum(bestcol[b], over_cols)

    def arrived(k):
        pair(k, k, True)

        @pl.loop(0, k)
        def _(b):
            pair(b, k, False)

    rows[NZ - 1] = recv1[z].reshape(BLK, PC)
    pair(NZ - 1, NZ - 1, True)

    @pl.loop(0, NZ - 1)
    def _(k):
        wait_bytes(recv2.at[k], rz_r.at[k])
        rows[k] = recv2[k].reshape(BLK, PC)
        arrived(k)
        pair(NZ - 1, k, False)

    for k, step in enumerate(ORDER):
        final = jnp.maximum(
            jnp.max(best[k], axis=0, keepdims=True), jnp.max(bestcol[k].T, axis=0, keepdims=True)
        )
        ret_row[k] = final
        z2 = lax.rem(z + NZ - step, NZ)
        if step:
            pltpu.make_async_remote_copy(
                src_ref=ret_row.at[k], dst_ref=ret_z.at[z], send_sem=bz_s, recv_sem=bz_r,
                device_id=at_z(z2), device_id_type=MESH,
            ).start()
        else:
            ret_z[z] = final
    wait_bytes(ret_z.at[pl.ds(0, NZ - 1)], bz_r)
    ret_p[...] = jnp.concatenate(
        [ret_z[...].reshape(NZ, BLK), jnp.zeros((128 - NZ, BLK), f32)], axis=0
    ).T.reshape(NP, DEPTH, 128)

    @pl.loop(1, NP)
    def _(step):
        p2 = turn_p(step)
        pltpu.make_async_remote_copy(
            src_ref=ret_p.at[p2], dst_ref=ret_c.at[p], send_sem=bp_s, recv_sem=bp_r,
            device_id=at_p(p2), device_id_type=MESH,
        ).start()

    ret_c[p] = ret_p[p]
    wait_bytes(ret_c.at[pl.ds(0, NP - 1)], bp_r)
    whole = ret_c[...].reshape(BLK, 128).T[:NZ, :]
    high = whole.astype(bf16)
    rest = whole - high.astype(f32)
    mid = rest.astype(bf16)
    low = (rest - mid.astype(f32)).astype(bf16)
    got = jnp.zeros((NZ, ROWS), f32)
    for piece in (high, mid, low):
        got = got + jnp.dot(piece, place[...], preferred_element_type=f32)
    slots = slot_ref[...]
    mask = lax.broadcasted_iota(i32, (NZ, ROWS), 0) == slots // BLK
    out_ref[...] = jnp.sum(jnp.where(mask, got, 0.0), axis=0, keepdims=True)

    wait_bytes(idx_p.at[pl.ds(0, NP - 1)], ip_s)
    wait_bytes(idx_z.at[pl.ds(0, NZ - 1)], iz_s)
    wait_bytes(send.at[:, pl.ds(0, NP - 1)], rp_s)
    for k, step in enumerate(ORDER):
        if step:
            wait_bytes(recv1.at[k], rz_s.at[k])
    wait_bytes(ret_row.at[pl.ds(0, NZ - 1)], bz_s)
    wait_bytes(ret_p.at[pl.ds(0, NP - 1)], bp_s)


def on_device(embeddings, pca_basis, cluster, doc_index):
    vmem = pl.BlockSpec(memory_space=pltpu.VMEM)
    hbm = pl.BlockSpec(memory_space=pl.ANY)
    dma = pltpu.SemaphoreType.DMA
    out = pl.pallas_call(
        kernel,
        out_shape=jax.ShapeDtypeStruct((1, ROWS), f32),
        in_specs=[vmem, vmem, hbm, hbm],
        out_specs=vmem,
        scratch_shapes=[
            pltpu.VMEM((NEMB, EROWS, E), bf16),
            pltpu.VMEM((E, PC), bf16),
            pltpu.VMEM((ROWS, PC), bf16),
            pltpu.VMEM((BLK, ROWS), bf16),
            pltpu.VMEM((ROWS, ROWS), bf16),
            pltpu.VMEM((1, ROWS), i32),
            pltpu.VMEM((128, ROWS), bf16),
            pltpu.VMEM((NP, DEPTH, 128), f32),
            pltpu.VMEM((NP, DEPTH, 128), f32),
            pltpu.VMEM((NZ, 1, BLK), f32),
            pltpu.VMEM((NZ, 1, BLK), f32),
            pltpu.VMEM((NZ, BLK, 128), f32),
            pltpu.VMEM((NZ, NP, DEPTH, PC), bf16),
            pltpu.VMEM((NZ, NP, DEPTH, PC), bf16),
            pltpu.VMEM((NZ, NP, DEPTH, PC), bf16),
            pltpu.VMEM((NZ, BLK, PC), bf16),
            pltpu.VMEM((NZ, 8, BLK), f32),
            pltpu.VMEM((NZ, BLK, 128), f32),
            pltpu.VMEM((NZ, 1, BLK), f32),
            pltpu.VMEM((NZ, 1, BLK), f32),
            pltpu.VMEM((NP, DEPTH, 128), f32),
            pltpu.VMEM((NP, DEPTH, 128), f32),
            dma((NEMB,)), dma, dma, dma, dma, dma, dma, dma((NZ,)), dma((NZ,)), dma((NZ,)),
            dma, dma, dma, dma,
        ],
        compiler_params=pltpu.CompilerParams(
            collective_id=0, has_side_effects=True, vmem_limit_bytes=60 * 2**20
        ),
    )(cluster.reshape(1, ROWS), doc_index.reshape(1, ROWS), embeddings, pca_basis)
    return out.reshape(ROWS)


def solution(mesh):
    return jax.shard_map(
        on_device,
        mesh=mesh,
        in_specs=(P(("docs", "rep"), None), P(), P(("docs", "rep"), None), P(("docs", "rep"))),
        out_specs=P(("docs", "rep")),
        check_vma=False,
    )
```

time: 115 us -> 65.8 us (0.57)
  Pallas kernels: 0 us -> 64.3 us
  waiting for transfers between devices: 45.8 us -> 0 us
  starting transfers between devices: 34.5 us -> 0 us
  local copies, waits for them, and re-layouts: 23.1 us -> 1.28 us
  matrix products: 10.1 us -> 0 us
    pallas_call x0 -> x1, Pallas kernels: none -> 64.3 us  [on_device(): pl.pallas_call(kernel, out_shape=jax.ShapeDtypeStruct((1, ROWS), f32), in...]
    all_to_all x3 -> x0, waiting for transfers between devices: 45.8 us -> none  [exchange_both(): lax.all_to_all(pieces, axis, split_axis=0, concat_axis=0, tiled=True)]
    all_to_all x3 -> x0, starting transfers between devices: 34.5 us -> none  [exchange_both(): lax.all_to_all(pieces, axis, split_axis=0, concat_axis=0, tiled=True)]
    gather x1 -> x0, local copies, waits for them, and re-layouts: 10.5 us -> none  [on_device(): nearest = returned.reshape(-1)[slot_of]]
    scatter x2 -> x0, local copies, waits for them, and re-layouts: 10.5 us -> none  [the longest x1 6.03 us: on_device(): jnp.zeros((clusters * slot_depth, features), jnp.bfloat16).at[slot_of]]
    dot_general x3 -> x0, matrix products: 10.1 us -> none  [the longest x1 5.76 us: on_device(): jnp.dot(embeddings, pca_basis, preferred_element_type=jnp.float32)]
    another operation x3 -> x0, local copies, waits for them, and re-layouts: 1.64 us -> none  [the longest x2 1.48 us: exchange_both(): pieces = pieces.reshape(-1, *inside)]
    unnamed x2 -> x1, local copies, waits for them, and re-layouts: 0.01 us -> 1.28 us
  transfers between devices with their start and end apart: 3 -> 0, of which waited for: 3 -> 0; matrix products, arithmetic and copies ran while one was open for 11% -> 0% of each run, Pallas kernels for 0% -> 0%
where the time goes in v1:
time: 65.8 us; the launch traced here: 65.6 us
  Pallas kernels  64.3 us (98%)
  local copies, waits for them, and re-layouts  1.28 us (2%)
    pallas_call x1, Pallas kernels, on_device(): pl.pallas_call(kernel, out_shape=jax.ShapeDtypeStruct((1, ROWS), f32), in...  64.3 us

profile of v1, /device:TPU:1, one launch (start us, length us, event | category | flops | bytes accessed | tf_op | source)
XLA Modules:
  0.0 65.6 jit_solution(16990874756663616508)
XLA Ops:
  0.0 64.3 %shard_map.46 = f32[1,1024]{1,0:T(1,128)} custom-call(s32[1,1024]{1,0:T(1,128)} %bitcast.4, s32[1,1024]{1,0:T(1,128)} %bitcast.5, bf16[1024,4096]{1,0:T(8,128)(2,1)} %emb_ref.1, bf16[4096,256]{1,0:T(8,128)(2,1)} %bas_ref.1), custom_call_target="tpu_custom_call" | custom-call | tf_op jit(solution)/shard_map/pallas_call | solution.py:254
  64.3 1.3 %copy.6 = f32[1024]{0:T(1024)} copy(f32[1024]{0:T(1024)} %bitcast.3) | data formatting | bytes 8192

commit v2 on v1

v2 whole, which is shorter than its diff:
```python
import jax
import jax.numpy as jnp
from jax import lax
from jax.experimental import pallas as pl
from jax.experimental.pallas import tpu as pltpu
from jax.sharding import PartitionSpec as P

MESH = pl.DeviceIdType.MESH
NX, NY, NZ, NC = 4, 4, 8, 2
NP = NX * NY * NC
DEPTH = 8
ROWS = 1024
PC = 256
E = 4096
BLK = NP * DEPTH
NEMB = 8
DEEP = E // NEMB
EROWS = 256
FAR = (4,)
NEAR = (3, 5, 2, 6, 1, 7)
ORDER = (0, 3, 5, 4, 2, 6, 1, 7)
BIG = float(2**30)
f32, bf16, i32 = jnp.float32, jnp.bfloat16, jnp.int32


def dot(a, b, ca, cb):
    return lax.dot_general(a, b, (((ca,), (cb,)), ((), ())), preferred_element_type=f32)


def wait_bytes(ref, sem):
    pltpu.make_async_copy(ref, ref, sem).wait()


def kernel(
    cl_ref, ix_ref, emb_ref, bas_ref, out_ref,
    ebuf, bbuf, proj, unit, which, upper, slot_ref,
    idx_p, idx_in, idx_z, idx_rec, col,
    send, recv1, zin, fin, rows, best, bestcol,
    ret_row, ret_z, ret_p, ret_c,
    e_sem, b_sem, ip_s, ip_r, iz_s, iz_r, rp_s, rp_r, zi_s, zi_r, fw_s, fin_r, rz_s,
    bz_s, bz_r, bp_s, bp_r,
):
    d = lax.axis_index("docs")
    y = lax.axis_index("rep")
    core = lax.rem(d, NC)
    z = lax.rem(d // NC, NZ)
    x = d // (NC * NZ)
    p = (x * NY + y) * NC + core

    def at_z(z2):
        return ((x * NZ + z2) * NC + core, y)

    def at_p(p2):
        return (((p2 // (NY * NC)) * NZ + z) * NC + lax.rem(p2, NC), lax.rem(p2 // NC, NY))

    def turn_z(step):
        return lax.rem(z + step, NZ)

    def turn_p(step):
        return lax.rem(p + step, NP)

    def to_z(src, dst, send_sem, recv_sem, z2):
        pltpu.make_async_remote_copy(
            src_ref=src, dst_ref=dst, send_sem=send_sem, recv_sem=recv_sem,
            device_id=at_z(z2), device_id_type=MESH,
        ).start()

    def to_plane(src, dst, send_sem, recv_sem):
        @pl.loop(1, NP)
        def _(step):
            p2 = turn_p(step)
            pltpu.make_async_remote_copy(
                src_ref=src.at[p2], dst_ref=dst.at[p], send_sem=send_sem, recv_sem=recv_sem,
                device_id=at_p(p2), device_id_type=MESH,
            ).start()

        dst[p] = src[p]

    def all_but_one(ref):
        return ref.at[pl.ds(0, NP - 1)]


    def depth_in(n):
        part = pl.ds(n * DEEP, DEEP)
        return (
            pltpu.make_async_copy(bas_ref.at[part], bbuf.at[part], b_sem.at[n]),
            pltpu.make_async_copy(emb_ref.at[:, part], ebuf.at[:, part], e_sem.at[n]),
        )

    for n in range(NEMB):
        for copy in depth_in(n):
            copy.start()
    barrier = pltpu.get_barrier_semaphore()
    for step in range(1, NZ):
        pl.semaphore_signal(barrier, inc=1, device_id=at_z(turn_z(step)), device_id_type=MESH)

    @pl.loop(1, NP)
    def _(step):
        pl.semaphore_signal(barrier, inc=1, device_id=at_p(turn_p(step)), device_id_type=MESH)

    cl = cl_ref[...]
    one_hot = (lax.broadcasted_iota(i32, (NZ * NP, ROWS), 0) == cl).astype(f32)
    upper[...] = (
        lax.broadcasted_iota(i32, (ROWS, ROWS), 0) < lax.broadcasted_iota(i32, (ROWS, ROWS), 1)
    ).astype(f32).astype(bf16)
    earlier = dot(one_hot.astype(bf16), upper[...], 1, 0)
    rank = jnp.sum(earlier * one_hot, axis=0, keepdims=True).astype(i32)
    slot_ref[...] = cl * DEPTH + rank
    lane = rank * NZ + cl // NP
    which[...] = (lax.broadcasted_iota(i32, (NP, ROWS), 0) == lax.rem(cl, NP)).astype(f32).astype(bf16)
    number = ix_ref[...] + 1
    mine = lax.broadcasted_iota(i32, (128, ROWS), 0) == lane
    total = jnp.zeros((NP, 128), f32)
    for part, weight in ((number // 4096, 4096.0), (lax.rem(number // 64, 64), 64.0), (lax.rem(number, 64), 1.0)):
        held = jnp.where(mine, part.astype(f32), 0.0).astype(bf16)
        total = total + weight * dot(which[...], held, 1, 1)
    idx_p[...] = total.reshape(NP, 1, 128)

    for n in range(NEMB):
        for copy in depth_in(n):
            copy.wait()
        part = slice(n * DEEP, (n + 1) * DEEP)
        partial = jnp.dot(ebuf[:, part], bbuf[part, :], preferred_element_type=f32)
        proj[...] = proj[...] + partial if n else partial
    for n in range(ROWS // EROWS):
        part = slice(n * EROWS, (n + 1) * EROWS)
        projected = proj[part, :]
        scale = lax.rsqrt(jnp.sum(projected * projected, axis=1, keepdims=True) + 1e-06)
        unit[part, :] = (projected * scale).astype(bf16)

    def put(step):
        z2 = turn_z(step)
        picks = (lax.broadcasted_iota(i32, (BLK, ROWS), 0) == slot_ref[...] - z2 * BLK).astype(f32)
        chosen = jnp.dot(picks.astype(bf16), unit[...], preferred_element_type=f32)
        send[z2] = chosen.reshape(NP, DEPTH, PC).astype(bf16)

    pl.semaphore_wait(barrier, NZ - 1 + NP - 1)

    def own_lanes():
        return lax.broadcasted_iota(i32, (BLK, 128), 1) // NZ == lax.rem(
            lax.broadcasted_iota(i32, (BLK, 128), 0), DEPTH
        )

    def pass_numbers():
        wait_bytes(all_but_one(idx_in), ip_r)
        wide = jnp.broadcast_to(idx_in[...], (NP, DEPTH, 128)).reshape(BLK, 128)
        keep = own_lanes()
        turned = jnp.where(keep, wide, 0.0).T.reshape(128 // NZ, NZ, BLK).sum(axis=0)
        for k in range(NZ):
            idx_z[k] = turned[k : k + 1, :]
        for k, step in enumerate(ORDER):
            if step:
                to_z(idx_z.at[turn_z(step)], idx_rec.at[k], iz_s, iz_r, turn_z(step))
            else:
                idx_rec[k] = idx_z[z]

    def onward(step):
        k = ORDER.index(step)
        z2 = turn_z(step)
        wait_bytes(all_but_one(recv1.at[z2]), rp_r.at[z2])
        to_z(recv1.at[z2], fin.at[k], rz_s.at[k], fin_r.at[k], z2)

    def across(step):
        j, k = FAR.index(step), ORDER.index(step)
        wait_bytes(zin.at[j], zi_r.at[j])
        to_plane(zin.at[j], fin.at[k], fw_s, fin_r.at[k])

    def spread_put(step):
        put(step)
        z2 = turn_z(step)
        to_plane(send.at[z2], recv1.at[z2], rp_s, rp_r.at[z2])

    put(FAR[0])
    to_z(send.at[turn_z(FAR[0])], zin.at[0], zi_s.at[0], zi_r.at[0], turn_z(FAR[0]))
    spread_put(3)
    to_plane(idx_p, idx_in, ip_s, ip_r)
    spread_put(5)
    spread_put(2)
    spread_put(6)
    pass_numbers()
    onward(3)
    spread_put(1)
    onward(5)
    spread_put(7)
    onward(2)
    spread_put(0)
    across(4)
    onward(6)
    onward(1)
    onward(7)

    wait_bytes(idx_rec.at[pl.ds(0, NZ - 1)], iz_r)

    @pl.loop(0, NZ)
    def _(k):
        row = idx_rec[k]
        row = jnp.where(row == 0.0, BIG, row)
        idx_rec[k] = row
        col[k] = jnp.broadcast_to(row, (128, BLK)).T
        best[k] = jnp.full((8, BLK), -1.0, f32)
        bestcol[k] = jnp.full((BLK, 128), -1.0, f32)

    def pair(b, a, same):
        scores = dot(rows[b], rows[a], 1, 1)
        cb = col[b]
        ra = idx_rec[a]
        over_rows = []
        over_cols = None
        for h in range(BLK // 128):
            lanes = slice(h * 128, (h + 1) * 128)
            s = scores[:, lanes]
            allowed = cb < ra[:, lanes]
            over_rows.append(jnp.max(jnp.where(allowed, s, -1.0).reshape(BLK // 8, 8, 128), axis=0))
            if not same:
                other = jnp.where(allowed, -1.0, s)
                over_cols = other if over_cols is None else jnp.maximum(over_cols, other)
        best[a] = jnp.maximum(best[a], jnp.concatenate(over_rows, axis=1))
        if not same:
            bestcol[b] = jnp.maximum(bestcol[b], over_cols)

    def meet(k):
        pair(k, k, True)
        for b in range(k):
            pair(b, k, False)

    for k, step in enumerate(ORDER):
        if step == 0:
            wait_bytes(all_but_one(recv1.at[z]), rp_r.at[z])
            rows[k] = recv1[z].reshape(BLK, PC)
        else:
            if step in FAR:
                wait_bytes(all_but_one(fin.at[k]), fin_r.at[k])
            else:
                wait_bytes(fin.at[k], fin_r.at[k])
            rows[k] = fin[k].reshape(BLK, PC)
        meet(k)

    finals = [
        jnp.maximum(
            jnp.max(best[k], axis=0, keepdims=True), jnp.max(bestcol[k].T, axis=0, keepdims=True)
        )
        for k in range(NZ)
    ]
    for k in range(1, NZ):
        ret_row[k] = finals[k]
    for k in range(1, NZ):
        to_z(ret_row.at[k], ret_z.at[z], bz_s, bz_r, turn_z(NZ - ORDER[k]))
    ret_z[z] = finals[0]
    wait_bytes(ret_z.at[pl.ds(0, NZ - 1)], bz_r)
    stacked = ret_z[...].reshape(NZ, BLK)
    spread = jnp.concatenate([stacked] * (128 // NZ), axis=0).T
    ret_p[...] = jnp.where(own_lanes(), spread, 0.0).reshape(NP, DEPTH, 128).sum(axis=1, keepdims=True)
    to_plane(ret_p, ret_c, bp_s, bp_r)
    wait_bytes(all_but_one(ret_c), bp_r)
    whole = ret_c[...].reshape(NP, 128).T[: NZ * DEPTH, :]
    high = whole.astype(bf16)
    rest = whole - high.astype(f32)
    mid = rest.astype(bf16)
    low = (rest - mid.astype(f32)).astype(bf16)
    got = jnp.zeros((NZ * DEPTH, ROWS), f32)
    for piece in (high, mid, low):
        got = got + jnp.dot(piece, which[...], preferred_element_type=f32)
    slots = slot_ref[...]
    lanes = lax.rem(slots, DEPTH) * NZ + slots // BLK
    mask = lax.broadcasted_iota(i32, (NZ * DEPTH, ROWS), 0) == lanes
    out_ref[...] = jnp.sum(jnp.where(mask, got, 0.0), axis=0, keepdims=True)

    wait_bytes(all_but_one(idx_p), ip_s)
    wait_bytes(idx_z.at[pl.ds(0, NZ - 1)], iz_s)
    wait_bytes(send.at[pl.ds(0, len(NEAR) + 1), pl.ds(0, NP - 1)], rp_s)
    for j in range(len(FAR)):
        wait_bytes(zin.at[j], zi_s.at[j])
    wait_bytes(zin.at[:, pl.ds(0, NP - 1)], fw_s)
    for step in NEAR:
        k = ORDER.index(step)
        wait_bytes(fin.at[k], rz_s.at[k])
    wait_bytes(ret_row.at[pl.ds(0, NZ - 1)], bz_s)
    wait_bytes(all_but_one(ret_p), bp_s)


def on_device(embeddings, pca_basis, cluster, doc_index):
    vmem = pl.BlockSpec(memory_space=pltpu.VMEM)
    hbm = pl.BlockSpec(memory_space=pl.ANY)
    dma = pltpu.SemaphoreType.DMA
    out = pl.pallas_call(
        kernel,
        out_shape=jax.ShapeDtypeStruct((1, ROWS), f32),
        in_specs=[vmem, vmem, hbm, hbm],
        out_specs=vmem,
        scratch_shapes=[
            pltpu.VMEM((ROWS, E), bf16),
            pltpu.VMEM((E, PC), bf16),
            pltpu.VMEM((ROWS, PC), f32),
            pltpu.VMEM((ROWS, PC), bf16),
            pltpu.VMEM((NP, ROWS), bf16),
            pltpu.VMEM((ROWS, ROWS), bf16),
            pltpu.VMEM((1, ROWS), i32),
            pltpu.VMEM((NP, 1, 128), f32),
            pltpu.VMEM((NP, 1, 128), f32),
            pltpu.VMEM((NZ, 1, BLK), f32),
            pltpu.VMEM((NZ, 1, BLK), f32),
            pltpu.VMEM((NZ, BLK, 128), f32),
            pltpu.VMEM((NZ, NP, DEPTH, PC), bf16),
            pltpu.VMEM((NZ, NP, DEPTH, PC), bf16),
            pltpu.VMEM((len(FAR), NP, DEPTH, PC), bf16),
            pltpu.VMEM((NZ, NP, DEPTH, PC), bf16),
            pltpu.VMEM((NZ, BLK, PC), bf16),
            pltpu.VMEM((NZ, 8, BLK), f32),
            pltpu.VMEM((NZ, BLK, 128), f32),
            pltpu.VMEM((NZ, 1, BLK), f32),
            pltpu.VMEM((NZ, 1, BLK), f32),
            pltpu.VMEM((NP, 1, 128), f32),
            pltpu.VMEM((NP, 1, 128), f32),
            dma((NEMB,)), dma((NEMB,)), dma, dma, dma, dma, dma, dma((NZ,)), dma((len(FAR),)), dma((len(FAR),)),
            dma, dma((NZ,)), dma((NZ,)), dma, dma, dma, dma,
        ],
        compiler_params=pltpu.CompilerParams(
            collective_id=0, has_side_effects=True, vmem_limit_bytes=60 * 2**20
        ),
    )(cluster.reshape(1, ROWS), doc_index.reshape(1, ROWS), embeddings, pca_basis)
    return out.reshape(ROWS)


def solution(mesh):
    return jax.shard_map(
        on_device,
        mesh=mesh,
        in_specs=(P(("docs", "rep"), None), P(), P(("docs", "rep"), None), P(("docs", "rep"))),
        out_specs=P(("docs", "rep")),
        check_vma=False,
    )
```

time: 65.8 us -> 54.7 us (0.83)
  Pallas kernels: 64.3 us -> 53.2 us
    pallas_call x1, Pallas kernels: 64.3 us -> 53.2 us  [on_device(): pl.pallas_call(kernel, out_shape=jax.ShapeDtypeStruct((1, ROWS), f32), in...]
where the time goes in v2:
time: 54.7 us; the launch traced here: 54.5 us
  Pallas kernels  53.2 us (97%)
  local copies, waits for them, and re-layouts  1.28 us (2%)
    pallas_call x1, Pallas kernels, on_device(): pl.pallas_call(kernel, out_shape=jax.ShapeDtypeStruct((1, ROWS), f32), in...  53.2 us
    unnamed x1, local copies, waits for them, and re-layouts  1.28 us

profile of v2, /device:TPU:1, one launch (start us, length us, event | category | flops | bytes accessed | tf_op | source)
XLA Modules:
  0.0 54.5 jit_solution(1331043720531529405)
XLA Ops:
  0.0 53.2 %shard_map.46 = f32[1,1024]{1,0:T(1,128)} custom-call(s32[1,1024]{1,0:T(1,128)} %bitcast.4, s32[1,1024]{1,0:T(1,128)} %bitcast.5, bf16[1024,4096]{1,0:T(8,128)(2,1)} %emb_ref.1, bf16[4096,256]{1,0:T(8,128)(2,1)} %bas_ref.1), custom_call_target="tpu_custom_call" | custom-call | tf_op jit(solution)/shard_map/pallas_call | solution.py:285
  53.2 1.3 %copy.6 = f32[1024]{0:T(1024)} copy(f32[1024]{0:T(1024)} %bitcast.3) | data formatting | bytes 8192

commit v3 on v2

v3 whole, which is shorter than its diff:
```python
import jax
import jax.numpy as jnp
from jax import lax
from jax.experimental import pallas as pl
from jax.experimental.pallas import tpu as pltpu
from jax.sharding import PartitionSpec as P

MESH = pl.DeviceIdType.MESH
NX, NY, NZ, NC = 4, 4, 8, 2
NP = NX * NY * NC
DEPTH = 8
ROWS = 1024
PC = 256
E = 4096
BLK = NP * DEPTH
NEMB = 8
EARLY = 0
DEEP = E // NEMB
EROWS = 256
ORDER = (0, 3, 5, 4, 2, 6, 1, 7)
FAR = 3
BIG = float(2**30)
f32, bf16, i32 = jnp.float32, jnp.bfloat16, jnp.int32


def dot(a, b, ca, cb):
    return lax.dot_general(a, b, (((ca,), (cb,)), ((), ())), preferred_element_type=f32)


def step_of(j):
    return NZ // 2 + (1 - 2 * (j % 2)) * ((j + 1) // 2)


def slot_of(j):
    return j + (j + 5) // 8


def wait_bytes(ref, sem):
    pltpu.make_async_copy(ref, ref, sem).wait()


def kernel(
    cl_hbm, ix_hbm, emb_ref, bas_ref, out_ref,
    cl_ref, ix_ref, ebuf, bbuf, proj, unit, which, upper, slot_ref,
    idx_p, idx_in, idx_z, idx_rec, col, colnow,
    send, recv1, zin, fin, rows, best, bestcol,
    ret_row, ret_z, ret_p, ret_c,
    n_sem, e_sem, b_sem, ip_s, ip_r, iz_s, iz_r, rp_s, rp_r, zi_s, zi_r, fw_s, fin_r, rz_s,
    bz_s, bz_r, bp_s, bp_r,
):
    d = lax.axis_index("docs")
    y = lax.axis_index("rep")
    core = lax.rem(d, NC)
    z = lax.rem(d // NC, NZ)
    x = d // (NC * NZ)
    p = (x * NY + y) * NC + core

    def at_z(z2):
        return ((x * NZ + z2) * NC + core, y)

    def turn_z(step):
        return lax.rem(z + step, NZ)

    beside = [
        (lax.rem(y + ky, NY), lax.rem(core + kc, NC)) for ky in range(NY) for kc in range(NC)
    ]
    beside = [(y2, y2 * NC + c2, z * NC + c2) for y2, c2 in beside]

    def each_beside(fn):
        def of_column(x2, some):
            for y2, place, deep in some:
                fn(x2 * (NY * NC) + place, (x2 * (NZ * NC) + deep, y2))

        of_column(x, beside[1:])

        @pl.loop(1, NX)
        def _(kx):
            of_column(lax.rem(x + kx, NX), beside)

    def to_z(src, dst, send_sem, recv_sem, z2):
        pltpu.make_async_remote_copy(
            src_ref=src, dst_ref=dst, send_sem=send_sem, recv_sem=recv_sem,
            device_id=at_z(z2), device_id_type=MESH,
        ).start()

    def to_plane(src, dst, send_sem, recv_sem):
        def to_one(p2, device):
            pltpu.make_async_remote_copy(
                src_ref=src.at[p2], dst_ref=dst.at[p], send_sem=send_sem, recv_sem=recv_sem,
                device_id=device, device_id_type=MESH,
            ).start()

        each_beside(to_one)
        dst[p] = src[p]

    def all_but_one(ref):
        return ref.at[pl.ds(0, NP - 1)]

    cl_copy = pltpu.make_async_copy(cl_hbm, cl_ref, n_sem.at[0])
    ix_copy = pltpu.make_async_copy(ix_hbm, ix_ref, n_sem.at[1])
    cl_copy.start()
    ix_copy.start()
    def depth_in(n):
        part = pl.ds(pl.multiple_of(n * DEEP, DEEP), DEEP)
        return (
            pltpu.make_async_copy(bas_ref.at[part], bbuf.at[part], b_sem.at[n]),
            pltpu.make_async_copy(emb_ref.at[:, part], ebuf.at[:, part], e_sem.at[n]),
        )

    for n in range(EARLY):
        for copy in depth_in(n):
            copy.start()
    barrier = pltpu.get_barrier_semaphore()
    for step in range(1, NZ):
        pl.semaphore_signal(barrier, inc=1, device_id=at_z(turn_z(step)), device_id_type=MESH)

    each_beside(
        lambda p2, device: pl.semaphore_signal(barrier, inc=1, device_id=device, device_id_type=MESH)
    )

    cl_copy.wait()
    ix_copy.wait()
    for n in range(EARLY, NEMB):
        for copy in depth_in(n):
            copy.start()
    cl = cl_ref[...]
    one_hot = (lax.broadcasted_iota(i32, (NZ * NP, ROWS), 0) == cl).astype(f32)
    upper[...] = (
        lax.broadcasted_iota(i32, (ROWS, ROWS), 0) < lax.broadcasted_iota(i32, (ROWS, ROWS), 1)
    ).astype(f32).astype(bf16)
    earlier = dot(one_hot.astype(bf16), upper[...], 1, 0)
    rank = jnp.sum(earlier * one_hot, axis=0, keepdims=True).astype(i32)
    slot_ref[...] = cl * DEPTH + rank
    lane = rank * NZ + cl // NP
    which[...] = (lax.broadcasted_iota(i32, (NP, ROWS), 0) == lax.rem(cl, NP)).astype(f32).astype(bf16)
    number = ix_ref[...] + 1
    mine = lax.broadcasted_iota(i32, (128, ROWS), 0) == lane
    total = jnp.zeros((NP, 128), f32)
    for part, weight in ((number // 4096, 4096.0), (lax.rem(number // 64, 64), 64.0), (lax.rem(number, 64), 1.0)):
        held = jnp.where(mine, part.astype(f32), 0.0).astype(bf16)
        total = total + weight * dot(which[...], held, 1, 1)
    idx_p[...] = total.reshape(NP, 1, 128)

    proj[...] = jnp.zeros((ROWS, PC), f32)

    @pl.loop(0, NEMB)
    def _(n):
        for copy in depth_in(n):
            copy.wait()
        part = pl.ds(pl.multiple_of(n * DEEP, DEEP), DEEP)
        proj[...] += jnp.dot(ebuf[:, part], bbuf[part, :], preferred_element_type=f32)

    for n in range(ROWS // EROWS):
        part = slice(n * EROWS, (n + 1) * EROWS)
        projected = proj[part, :]
        scale = lax.rsqrt(jnp.sum(projected * projected, axis=1, keepdims=True) + 1e-06)
        unit[part, :] = (projected * scale).astype(bf16)

    pl.semaphore_wait(barrier, NZ - 1 + NP - 1)

    def own_lanes():
        return lax.broadcasted_iota(i32, (BLK, 128), 1) // NZ == lax.rem(
            lax.broadcasted_iota(i32, (BLK, 128), 0), DEPTH
        )

    def pass_numbers():
        wait_bytes(all_but_one(idx_in), ip_r)
        wide = jnp.broadcast_to(idx_in[...], (NP, DEPTH, 128)).reshape(BLK, 128)
        keep = own_lanes()
        turned = jnp.where(keep, wide, 0.0).T.reshape(128 // NZ, NZ, BLK).sum(axis=0)
        for k in range(NZ):
            idx_z[k] = turned[k : k + 1, :]
        for k, step in enumerate(ORDER):
            if step:
                to_z(idx_z.at[turn_z(step)], idx_rec.at[k], iz_s, iz_r, turn_z(step))
            else:
                idx_rec[k] = idx_z[z]

    def onward(j):
        k = slot_of(j)
        z2 = turn_z(step_of(j))
        wait_bytes(all_but_one(recv1.at[z2]), rp_r.at[z2])
        to_z(recv1.at[z2], fin.at[k], rz_s.at[k], fin_r.at[k], z2)

    far = turn_z(ORDER[FAR])

    @pl.loop(0, NZ)
    def _(j):
        z2 = turn_z(step_of(j))
        picks = (lax.broadcasted_iota(i32, (BLK, ROWS), 0) == slot_ref[...] - z2 * BLK).astype(f32)
        chosen = jnp.dot(picks.astype(bf16), unit[...], preferred_element_type=f32)
        send[z2] = chosen.reshape(NP, DEPTH, PC).astype(bf16)

        @pl.when(j == 0)
        def _():
            to_z(send.at[far], zin, zi_s, zi_r, far)
            to_plane(idx_p, idx_in, ip_s, ip_r)

        @pl.when(j > 0)
        def _():
            to_plane(send.at[z2], recv1.at[z2], rp_s, rp_r.at[z2])

        @pl.when(j == 4)
        def _():
            pass_numbers()

        @pl.when(j >= 4)
        def _():
            onward(j - 3)

    wait_bytes(zin, zi_r)
    to_plane(zin, fin.at[FAR], fw_s, fin_r.at[FAR])

    @pl.loop(5, NZ - 1)
    def _(j):
        onward(j)

    wait_bytes(idx_rec.at[pl.ds(0, NZ - 1)], iz_r)

    @pl.loop(0, NZ)
    def _(k):
        row = idx_rec[k]
        row = jnp.where(row == 0.0, BIG, row)
        idx_rec[k] = row
        col[k] = jnp.broadcast_to(row, (128, BLK)).T
        colnow[k] = jnp.full((BLK, 128), BIG, f32)
        rows[k] = jnp.zeros((BLK, PC), bf16)
        bestcol[k] = jnp.full((BLK, 128), -1.0, f32)

    wait_bytes(all_but_one(recv1.at[z]), rp_r.at[z])
    fin[0] = recv1[z]

    @pl.loop(0, NZ)
    def _(k):
        @pl.when(k == FAR)
        def _():
            wait_bytes(all_but_one(fin.at[FAR]), fin_r.at[FAR])

        @pl.when(jnp.logical_and(k > 0, k != FAR))
        def _():
            wait_bytes(fin.at[k], fin_r.at[k])

        rows[k] = fin[k].reshape(BLK, PC)
        colnow[k] = col[k]
        ra = idx_rec[k]
        met = rows[k]
        over_rows = [None] * (BLK // 128)
        for b in range(NZ):
            scores = dot(rows[b], met, 1, 1)
            cb = colnow[b]
            over_cols = bestcol[b]
            for h in range(BLK // 128):
                lanes = slice(h * 128, (h + 1) * 128)
                s = scores[:, lanes]
                r = ra[:, lanes]
                earlier = cb < r
                own = jnp.max(jnp.where(earlier, s, -1.0).reshape(BLK // 8, 8, 128), axis=0)
                over_rows[h] = own if b == 0 else jnp.maximum(over_rows[h], own)
                over_cols = jnp.maximum(over_cols, jnp.where(earlier, -1.0, s))
            bestcol[b] = over_cols
        best[k] = jnp.concatenate(over_rows, axis=1)
        bestcol[k] = jnp.full((BLK, 128), -1.0, f32)

    finals = [
        jnp.maximum(
            jnp.max(best[k], axis=0, keepdims=True), jnp.max(bestcol[k].T, axis=0, keepdims=True)
        )
        for k in range(NZ)
    ]
    for k in range(1, NZ):
        ret_row[k] = finals[k]
    for k in range(1, NZ):
        to_z(ret_row.at[k], ret_z.at[z], bz_s, bz_r, turn_z(NZ - ORDER[k]))
    ret_z[z] = finals[0]
    wait_bytes(ret_z.at[pl.ds(0, NZ - 1)], bz_r)
    stacked = ret_z[...].reshape(NZ, BLK)
    spread = jnp.concatenate([stacked] * (128 // NZ), axis=0).T
    ret_p[...] = jnp.where(own_lanes(), spread, 0.0).reshape(NP, DEPTH, 128).sum(axis=1, keepdims=True)
    to_plane(ret_p, ret_c, bp_s, bp_r)
    wait_bytes(all_but_one(ret_c), bp_r)
    whole = ret_c[...].reshape(NP, 128).T[: NZ * DEPTH, :]
    high = whole.astype(bf16)
    rest = whole - high.astype(f32)
    mid = rest.astype(bf16)
    low = (rest - mid.astype(f32)).astype(bf16)
    got = jnp.zeros((NZ * DEPTH, ROWS), f32)
    for piece in (high, mid, low):
        got = got + jnp.dot(piece, which[...], preferred_element_type=f32)
    slots = slot_ref[...]
    lanes = lax.rem(slots, DEPTH) * NZ + slots // BLK
    mask = lax.broadcasted_iota(i32, (NZ * DEPTH, ROWS), 0) == lanes
    out_ref[...] = jnp.sum(jnp.where(mask, got, 0.0), axis=0, keepdims=True)

    wait_bytes(all_but_one(idx_p), ip_s)
    wait_bytes(idx_z.at[pl.ds(0, NZ - 1)], iz_s)
    wait_bytes(send.at[pl.ds(0, NZ - 1), pl.ds(0, NP - 1)], rp_s)
    wait_bytes(zin, zi_s)
    wait_bytes(all_but_one(zin), fw_s)
    for k in range(1, NZ):
        if k != FAR:
            wait_bytes(fin.at[k], rz_s.at[k])
    wait_bytes(ret_row.at[pl.ds(0, NZ - 1)], bz_s)
    wait_bytes(all_but_one(ret_p), bp_s)


def on_device(embeddings, pca_basis, cluster, doc_index):
    vmem = pl.BlockSpec(memory_space=pltpu.VMEM)
    hbm = pl.BlockSpec(memory_space=pl.ANY)
    dma = pltpu.SemaphoreType.DMA
    out = pl.pallas_call(
        kernel,
        out_shape=jax.ShapeDtypeStruct((1, ROWS), f32),
        in_specs=[hbm, hbm, hbm, hbm],
        out_specs=vmem,
        scratch_shapes=[
            pltpu.VMEM((1, ROWS), i32),
            pltpu.VMEM((1, ROWS), i32),
            pltpu.VMEM((ROWS, E), bf16),
            pltpu.VMEM((E, PC), bf16),
            pltpu.VMEM((ROWS, PC), f32),
            pltpu.VMEM((ROWS, PC), bf16),
            pltpu.VMEM((NP, ROWS), bf16),
            pltpu.VMEM((ROWS, ROWS), bf16),
            pltpu.VMEM((1, ROWS), i32),
            pltpu.VMEM((NP, 1, 128), f32),
            pltpu.VMEM((NP, 1, 128), f32),
            pltpu.VMEM((NZ, 1, BLK), f32),
            pltpu.VMEM((NZ, 1, BLK), f32),
            pltpu.VMEM((NZ, BLK, 128), f32),
            pltpu.VMEM((NZ, BLK, 128), f32),
            pltpu.VMEM((NZ, NP, DEPTH, PC), bf16),
            pltpu.VMEM((NZ, NP, DEPTH, PC), bf16),
            pltpu.VMEM((NP, DEPTH, PC), bf16),
            pltpu.VMEM((NZ, NP, DEPTH, PC), bf16),
            pltpu.VMEM((NZ, BLK, PC), bf16),
            pltpu.VMEM((NZ, 8, BLK), f32),
            pltpu.VMEM((NZ, BLK, 128), f32),
            pltpu.VMEM((NZ, 1, BLK), f32),
            pltpu.VMEM((NZ, 1, BLK), f32),
            pltpu.VMEM((NP, 1, 128), f32),
            pltpu.VMEM((NP, 1, 128), f32),
            dma((2,)), dma((NEMB,)), dma((NEMB,)), dma, dma, dma, dma, dma, dma((NZ,)), dma, dma,
            dma, dma((NZ,)), dma((NZ,)), dma, dma, dma, dma,
        ],
        compiler_params=pltpu.CompilerParams(
            collective_id=0, has_side_effects=True, vmem_limit_bytes=60 * 2**20
        ),
    )(cluster.reshape(1, ROWS), doc_index.reshape(1, ROWS), embeddings, pca_basis)
    return out.reshape(ROWS)


def solution(mesh):
    return jax.shard_map(
        on_device,
        mesh=mesh,
        in_specs=(P(("docs", "rep"), None), P(), P(("docs", "rep"), None), P(("docs", "rep"))),
        out_specs=P(("docs", "rep")),
        check_vma=False,
    )
```

time: 54.7 us -> 52.7 us (0.963)
  Pallas kernels: 53.2 us -> 51.2 us
    pallas_call x1, Pallas kernels: 53.2 us -> 51.2 us  [on_device(): pl.pallas_call(kernel, out_shape=jax.ShapeDtypeStruct((1, ROWS), f32), in...]
where the time goes in v3:
time: 52.7 us; the launch traced here: 52.5 us
  Pallas kernels  51.2 us (97%)
  local copies, waits for them, and re-layouts  1.28 us (2%)
    pallas_call x1, Pallas kernels, on_device(): pl.pallas_call(kernel, out_shape=jax.ShapeDtypeStruct((1, ROWS), f32), in...  51.2 us
    unnamed x1, local copies, waits for them, and re-layouts  1.28 us

profile of v3, /device:TPU:1, one launch (start us, length us, event | category | flops | bytes accessed | tf_op | source)
XLA Modules:
  0.0 52.5 jit_solution(8907323599405123136)
XLA Ops:
  0.0 51.2 %shard_map.46 = f32[1,1024]{1,0:T(1,128)} custom-call(s32[1,1024]{1,0:T(1,128)} %bitcast.4, s32[1,1024]{1,0:T(1,128)} %bitcast.5, bf16[1024,4096]{1,0:T(8,128)(2,1)} %emb_ref.1, bf16[4096,256]{1,0:T(8,128)(2,1)} %bas_ref.1), custom_call_target="tpu_custom_call" | custom-call | tf_op jit(solution)/shard_map/pallas_call | solution.py:310
  51.2 1.3 %copy.6 = f32[1024]{0:T(1024)} copy(f32[1024]{0:T(1024)} %bitcast.3) | data formatting | bytes 8192

commit v4 on v3

--- a/solution.py
+++ b/solution.py
@@ -17,8 +17,9 @@
 EARLY = 0
 DEEP = E // NEMB
 EROWS = 256
-ORDER = (0, 3, 5, 4, 2, 6, 1, 7)
-FAR = 3
+ORDER = (0, 4, 2, 6, 3, 5, 1, 7)
+FAR = (1, 4, 5)
+NFAR = 3
 BIG = float(2**30)
 f32, bf16, i32 = jnp.float32, jnp.bfloat16, jnp.int32
 
@@ -32,7 +33,7 @@
 
 
 def slot_of(j):
-    return j + (j + 5) // 8
+    return j - 1 + 2 * (j // 5)
 
 
 def wait_bytes(ref, sem):
@@ -182,8 +183,6 @@
         wait_bytes(all_but_one(recv1.at[z2]), rp_r.at[z2])
         to_z(recv1.at[z2], fin.at[k], rz_s.at[k], fin_r.at[k], z2)
 
-    far = turn_z(ORDER[FAR])
-
     @pl.loop(0, NZ)
     def _(j):
         z2 = turn_z(step_of(j))
@@ -191,29 +190,30 @@
         chosen = jnp.dot(picks.astype(bf16), unit[...], preferred_element_type=f32)
         send[z2] = chosen.reshape(NP, DEPTH, PC).astype(bf16)
 
+        @pl.when(j < NFAR)
+        def _():
+            to_z(send.at[z2], zin.at[j], zi_s.at[j], zi_r.at[j], z2)
+
         @pl.when(j == 0)
         def _():
-            to_z(send.at[far], zin, zi_s, zi_r, far)
             to_plane(idx_p, idx_in, ip_s, ip_r)
 
-        @pl.when(j > 0)
+        @pl.when(j >= NFAR)
         def _():
             to_plane(send.at[z2], recv1.at[z2], rp_s, rp_r.at[z2])
 
-        @pl.when(j == 4)
+        @pl.when(j == 6)
         def _():
             pass_numbers()
 
-        @pl.when(j >= 4)
-        def _():
-            onward(j - 3)
-
-    wait_bytes(zin, zi_r)
-    to_plane(zin, fin.at[FAR], fw_s, fin_r.at[FAR])
-
-    @pl.loop(5, NZ - 1)
+
+    @pl.loop(NFAR, NZ - 1)
     def _(j):
         onward(j)
+
+    for j, k in enumerate(FAR):
+        wait_bytes(zin.at[j], zi_r.at[j])
+        to_plane(zin.at[j], fin.at[k], fw_s, fin_r.at[k])
 
     wait_bytes(idx_rec.at[pl.ds(0, NZ - 1)], iz_r)
 
@@ -232,11 +232,13 @@
 
     @pl.loop(0, NZ)
     def _(k):
-        @pl.when(k == FAR)
-        def _():
-            wait_bytes(all_but_one(fin.at[FAR]), fin_r.at[FAR])
-
-        @pl.when(jnp.logical_and(k > 0, k != FAR))
+        far = jnp.logical_or(k == FAR[0], jnp.logical_and(k >= FAR[1], k <= FAR[2]))
+
+        @pl.when(far)
+        def _():
+            wait_bytes(all_but_one(fin.at[k]), fin_r.at[k])
+
+        @pl.when(jnp.logical_and(k > 0, jnp.logical_not(far)))
         def _():
             wait_bytes(fin.at[k], fin_r.at[k])
 
@@ -293,11 +295,12 @@
 
     wait_bytes(all_but_one(idx_p), ip_s)
     wait_bytes(idx_z.at[pl.ds(0, NZ - 1)], iz_s)
-    wait_bytes(send.at[pl.ds(0, NZ - 1), pl.ds(0, NP - 1)], rp_s)
-    wait_bytes(zin, zi_s)
-    wait_bytes(all_but_one(zin), fw_s)
+    wait_bytes(send.at[pl.ds(0, NZ - NFAR), pl.ds(0, NP - 1)], rp_s)
+    for j in range(NFAR):
+        wait_bytes(zin.at[j], zi_s.at[j])
+    wait_bytes(zin.at[:, pl.ds(0, NP - 1)], fw_s)
     for k in range(1, NZ):
-        if k != FAR:
+        if k not in FAR:
             wait_bytes(fin.at[k], rz_s.at[k])
     wait_bytes(ret_row.at[pl.ds(0, NZ - 1)], bz_s)
     wait_bytes(all_but_one(ret_p), bp_s)
@@ -330,7 +333,7 @@
             pltpu.VMEM((NZ, BLK, 128), f32),
             pltpu.VMEM((NZ, NP, DEPTH, PC), bf16),
             pltpu.VMEM((NZ, NP, DEPTH, PC), bf16),
-            pltpu.VMEM((NP, DEPTH, PC), bf16),
+            pltpu.VMEM((NFAR, NP, DEPTH, PC), bf16),
             pltpu.VMEM((NZ, NP, DEPTH, PC), bf16),
             pltpu.VMEM((NZ, BLK, PC), bf16),
             pltpu.VMEM((NZ, 8, BLK), f32),
@@ -339,7 +342,7 @@
             pltpu.VMEM((NZ, 1, BLK), f32),
             pltpu.VMEM((NP, 1, 128), f32),
             pltpu.VMEM((NP, 1, 128), f32),
-            dma((2,)), dma((NEMB,)), dma((NEMB,)), dma, dma, dma, dma, dma, dma((NZ,)), dma, dma,
+            dma((2,)), dma((NEMB,)), dma((NEMB,)), dma, dma, dma, dma, dma, dma((NZ,)), dma((NFAR,)), dma((NFAR,)),
             dma, dma((NZ,)), dma((NZ,)), dma, dma, dma, dma,
         ],
         compiler_params=pltpu.CompilerParams(

time: 52.7 us -> 51.5 us (0.977)
  Pallas kernels: 51.2 us -> 50 us
    pallas_call x1, Pallas kernels: 51.2 us -> 50 us  [on_device(): pl.pallas_call(kernel, out_shape=jax.ShapeDtypeStruct((1, ROWS), f32), in...]
where the time goes in v4:
time: 51.5 us; the launch traced here: 51.3 us
  Pallas kernels  50 us (97%)
  local copies, waits for them, and re-layouts  1.28 us (2%)
    pallas_call x1, Pallas kernels, on_device(): pl.pallas_call(kernel, out_shape=jax.ShapeDtypeStruct((1, ROWS), f32), in...  50 us
    unnamed x1, local copies, waits for them, and re-layouts  1.28 us

profile of v4, /device:TPU:1, one launch (start us, length us, event | category | flops | bytes accessed | tf_op | source)
XLA Modules:
  0.0 51.3 jit_solution(13727947929607110335)
XLA Ops:
  0.0 50.0 %shard_map.46 = f32[1,1024]{1,0:T(1,128)} custom-call(s32[1,1024]{1,0:T(1,128)} %bitcast.4, s32[1,1024]{1,0:T(1,128)} %bitcast.5, bf16[1024,4096]{1,0:T(8,128)(2,1)} %emb_ref.1, bf16[4096,256]{1,0:T(8,128)(2,1)} %bas_ref.1), custom_call_target="tpu_custom_call" | custom-call | tf_op jit(solution)/shard_map/pallas_call | solution.py:313
  50.0 1.3 %copy.6 = f32[1024]{0:T(1024)} copy(f32[1024]{0:T(1024)} %bitcast.3) | data formatting | bytes 8192

commit v5 on v4

--- a/solution.py
+++ b/solution.py
@@ -13,8 +13,8 @@
 PC = 256
 E = 4096
 BLK = NP * DEPTH
-NEMB = 8
-EARLY = 0
+NEMB = 4
+EARLY = 1
 DEEP = E // NEMB
 EROWS = 256
 ORDER = (0, 4, 2, 6, 3, 5, 1, 7)

time: 51.5 us -> 50.9 us (0.988)
  Pallas kernels: 50 us -> 49.4 us
    pallas_call x1, Pallas kernels: 50 us -> 49.4 us  [on_device(): pl.pallas_call(kernel, out_shape=jax.ShapeDtypeStruct((1, ROWS), f32), in...]
where the time goes in v5:
time: 50.9 us; the launch traced here: 50.7 us
  Pallas kernels  49.4 us (97%)
  local copies, waits for them, and re-layouts  1.28 us (3%)
    pallas_call x1, Pallas kernels, on_device(): pl.pallas_call(kernel, out_shape=jax.ShapeDtypeStruct((1, ROWS), f32), in...  49.4 us
    unnamed x1, local copies, waits for them, and re-layouts  1.28 us

profile of v5, /device:TPU:1, one launch (start us, length us, event | category | flops | bytes accessed | tf_op | source)
XLA Modules:
  0.0 50.7 jit_solution(2915592834460885615)
XLA Ops:
  0.0 49.4 %shard_map.46 = f32[1,1024]{1,0:T(1,128)} custom-call(s32[1,1024]{1,0:T(1,128)} %bitcast.4, s32[1,1024]{1,0:T(1,128)} %bitcast.5, bf16[1024,4096]{1,0:T(8,128)(2,1)} %emb_ref.1, bf16[4096,256]{1,0:T(8,128)(2,1)} %bas_ref.1), custom_call_target="tpu_custom_call" | custom-call | tf_op jit(solution)/shard_map/pallas_call | solution.py:313
  49.5 1.3 %copy.6 = f32[1024]{0:T(1024)} copy(f32[1024]{0:T(1024)} %bitcast.3) | data formatting | bytes 8192
